TPU v7x, 32 devices: a whole 2x2x4 slice. The times are simulated.
32 devices in a mesh: row: 8 (over z, core), col: 4 (over y, x).
Axes of the slice: x: 2, y: 2, z: 4, core: 2. Of those that a mesh axis runs over, the one named last changes fastest.
Arguments:
- gradient: float32 [8192, 28672], P('row', 'col'), may hold values from -100 to 100
- residual: float32 [8192, 28672], P('row', 'col'), may hold values from -3 to 3
- q_init: float32 [4, 28672], P(None, 'col'), may hold values from -5 to 5
Outputs:
- q_factor: float32 [4, 28672], P(None, 'col')
- new_residual: float32 [8192, 28672], P('row', 'col')
All inputs are finite; a program needn't handle non-finite values.
Results may differ from a plain program's by a relative error of at most 0.00012.
Values sent between devices are 32-bit elements; how exact they have to be, the bound alone decides.
A program may use at most 128 MiB of HBM per device.

v0:
```python
import jax
import jax.numpy as jnp
from jax import lax
from jax.sharding import PartitionSpec as P

ITERS = 16


def sum_over_cols(partial_value):
    return lax.psum(partial_value, "col")


def shards(gradient, residual, q_init):
    highest = lax.Precision.HIGHEST
    merged = gradient + residual

    def iterate(step_index, carry):
        q_current, p_previous = carry
        p_partial = lax.dot_general(
            q_current,
            merged,
            (((1,), (1,)), ((), ())),
            precision=highest,
            preferred_element_type=jnp.float32,
        )
        p_factor = sum_over_cols(p_partial)
        gram_part = lax.dot_general(
            p_factor,
            p_factor,
            (((1,), (1,)), ((), ())),
            precision=highest,
            preferred_element_type=jnp.float32,
        )
        cross_part = jnp.dot(
            p_factor, merged, precision=highest, preferred_element_type=jnp.float32
        )
        gram, cross = lax.psum((gram_part, cross_part), "row")
        factor_low = jnp.linalg.cholesky(gram)
        p_basis = jax.scipy.linalg.solve_triangular(factor_low, p_factor, lower=True)
        q_next = jax.scipy.linalg.solve_triangular(factor_low, cross, lower=True)
        return (q_next, p_basis)

    start = (q_init, jnp.zeros((q_init.shape[0], merged.shape[0]), jnp.float32))
    q_factor, p_basis = lax.fori_loop(0, ITERS, iterate, start)
    approx = lax.dot_general(
        p_basis,
        q_factor,
        (((0,), (0,)), ((), ())),
        precision=highest,
        preferred_element_type=jnp.float32,
    )
    return (q_factor, merged - approx)


def solution(mesh):
    in_specs = (P("row", "col"), P("row", "col"), P(None, "col"))
    out_specs = (P(None, "col"), P("row", "col"))
    return jax.shard_map(shards, mesh=mesh, in_specs=in_specs, out_specs=out_specs, check_vma=False)
```

profile of v0, /device:TPU:1, one launch (start us, length us, event | category | flops | bytes accessed | tf_op | source)
XLA Modules:
  0.0 1912.1 jit_solution(13343573732617844287)
XLA Ops:
  7.2 30.9 %add.27 = f32[1024,7168]{1,0:T(8,128)} add(f32[1024,7168]{1,0:T(8,128)} %param.5, f32[1024,7168]{1,0:T(8,128)} %param.6) | non-fusion elementwise | flops 7340032 | bytes 88080384 | tf_op jit(solution)/shard_map/add | solution.py:15
  38.1 1837.0 %while.12 = (s32[]{:T(128)}, f32[4,7168]{1,0:T(4,128)S(1)}, f32[4,1024]{1,0:T(4,128)}, f32[1024,7168]{1,0:T(8,128)}, s32[]{:T(128)}) while((s32[]{:T(128)}, f32[4,7168]{1,0:T(4,128)S(1)}, f32[4,1024]{1,0:T(4,128)}, f32[1024,7168]{1,0:T(8,128)}, s32[]{:T(128)}) %tuple.27), condition=%wide.region_6.7_spmd, body=%wide.region_0.6_spmd.sunk | while | flops 706445440 | bytes 59982788 | solution.py:44
  117.1 35.7 %all-reduce.2.cloned.1.call-done = f32[4,7168]{1,0:T(4,128)} async-done(((f32[4,7168]{1,0:T(4,128)}), f32[4,7168]{1,0:T(4,128)}) %all-reduce.2.cloned.1.call-update) | async-done | bytes 114704 | tf_op jit(solution)/shard_map/while/body/eval_jaxpr/psum | solution.py:37
  154.1 27.1 %fusion.46 = f32[4,1024]{1,0:T(4,128)S(1)} fusion(f32[4,7168]{1,0:T(4,128)S(1)} %get-tuple-element.63, f32[1024,7168]{1,0:T(8,128)} %get-tuple-element.70), kind=kOutput, calls=%fused_computation.13.clone.1 | convolution fusion | flops 352321536 | bytes 29491200 | tf_op jit(solution)/shard_map/while/body/eval_jaxpr/dot_general | solution.py:19
  231.7 35.8 %all-reduce.2.cloned.1.call-done = f32[4,7168]{1,0:T(4,128)} async-done(((f32[4,7168]{1,0:T(4,128)}), f32[4,7168]{1,0:T(4,128)}) %all-reduce.2.cloned.1.call-update) | async-done | bytes 114704 | tf_op jit(solution)/shard_map/while/body/eval_jaxpr/psum | solution.py:37
  268.9 27.1 %fusion.46 = f32[4,1024]{1,0:T(4,128)S(1)} fusion(f32[4,7168]{1,0:T(4,128)S(1)} %get-tuple-element.63, f32[1024,7168]{1,0:T(8,128)} %get-tuple-element.70), kind=kOutput, calls=%fused_computation.13.clone.1 | convolution fusion | flops 352321536 | bytes 29491200 | tf_op jit(solution)/shard_map/while/body/eval_jaxpr/dot_general | solution.py:19
  346.5 35.8 %all-reduce.2.cloned.1.call-done = f32[4,7168]{1,0:T(4,128)} async-done(((f32[4,7168]{1,0:T(4,128)}), f32[4,7168]{1,0:T(4,128)}) %all-reduce.2.cloned.1.call-update) | async-done | bytes 114704 | tf_op jit(solution)/shard_map/while/body/eval_jaxpr/psum | solution.py:37
  461.3 35.8 %all-reduce.2.cloned.1.call-done = f32[4,7168]{1,0:T(4,128)} async-done(((f32[4,7168]{1,0:T(4,128)}), f32[4,7168]{1,0:T(4,128)}) %all-reduce.2.cloned.1.call-update) | async-done | bytes 114704 | tf_op jit(solution)/shard_map/while/body/eval_jaxpr/psum | solution.py:37
  498.4 27.1 %fusion.46 = f32[4,1024]{1,0:T(4,128)S(1)} fusion(f32[4,7168]{1,0:T(4,128)S(1)} %get-tuple-element.63, f32[1024,7168]{1,0:T(8,128)} %get-tuple-element.70), kind=kOutput, calls=%fused_computation.13.clone.1 | convolution fusion | flops 352321536 | bytes 29491200 | tf_op jit(solution)/shard_map/while/body/eval_jaxpr/dot_general | solution.py:19
  576.0 35.8 %all-reduce.2.cloned.1.call-done = f32[4,7168]{1,0:T(4,128)} async-done(((f32[4,7168]{1,0:T(4,128)}), f32[4,7168]{1,0:T(4,128)}) %all-reduce.2.cloned.1.call-update) | async-done | bytes 114704 | tf_op jit(solution)/shard_map/while/body/eval_jaxpr/psum | solution.py:37
  690.7 35.8 %all-reduce.2.cloned.1.call-done = f32[4,7168]{1,0:T(4,128)} async-done(((f32[4,7168]{1,0:T(4,128)}), f32[4,7168]{1,0:T(4,128)}) %all-reduce.2.cloned.1.call-update) | async-done | bytes 114704 | tf_op jit(solution)/shard_map/while/body/eval_jaxpr/psum | solution.py:37
  805.4 35.8 %all-reduce.2.cloned.1.call-done = f32[4,7168]{1,0:T(4,128)} async-done(((f32[4,7168]{1,0:T(4,128)}), f32[4,7168]{1,0:T(4,128)}) %all-reduce.2.cloned.1.call-update) | async-done | bytes 114704 | tf_op jit(solution)/shard_map/while/body/eval_jaxpr/psum | solution.py:37
  920.2 35.8 %all-reduce.2.cloned.1.call-done = f32[4,7168]{1,0:T(4,128)} async-done(((f32[4,7168]{1,0:T(4,128)}), f32[4,7168]{1,0:T(4,128)}) %all-reduce.2.cloned.1.call-update) | async-done | bytes 114704 | tf_op jit(solution)/shard_map/while/body/eval_jaxpr/psum | solution.py:37
  1034.9 35.8 %all-reduce.2.cloned.1.call-done = f32[4,7168]{1,0:T(4,128)} async-done(((f32[4,7168]{1,0:T(4,128)}), f32[4,7168]{1,0:T(4,128)}) %all-reduce.2.cloned.1.call-update) | async-done | bytes 114704 | tf_op jit(solution)/shard_map/while/body/eval_jaxpr/psum | solution.py:37
  1072.1 27.1 %fusion.46 = f32[4,1024]{1,0:T(4,128)S(1)} fusion(f32[4,7168]{1,0:T(4,128)S(1)} %get-tuple-element.63, f32[1024,7168]{1,0:T(8,128)} %get-tuple-element.70), kind=kOutput, calls=%fused_computation.13.clone.1 | convolution fusion | flops 352321536 | bytes 29491200 | tf_op jit(solution)/shard_map/while/body/eval_jaxpr/dot_general | solution.py:19
  1149.7 35.8 %all-reduce.2.cloned.1.call-done = f32[4,7168]{1,0:T(4,128)} async-done(((f32[4,7168]{1,0:T(4,128)}), f32[4,7168]{1,0:T(4,128)}) %all-reduce.2.cloned.1.call-update) | async-done | bytes 114704 | tf_op jit(solution)/shard_map/while/body/eval_jaxpr/psum | solution.py:37
  1264.4 35.8 %all-reduce.2.cloned.1.call-done = f32[4,7168]{1,0:T(4,128)} async-done(((f32[4,7168]{1,0:T(4,128)}), f32[4,7168]{1,0:T(4,128)}) %all-reduce.2.cloned.1.call-update) | async-done | bytes 114704 | tf_op jit(solution)/shard_map/while/body/eval_jaxpr/psum | solution.py:37
  1301.5 27.1 %fusion.46 = f32[4,1024]{1,0:T(4,128)S(1)} fusion(f32[4,7168]{1,0:T(4,128)S(1)} %get-tuple-element.63, f32[1024,7168]{1,0:T(8,128)} %get-tuple-element.70), kind=kOutput, calls=%fused_computation.13.clone.1 | convolution fusion | flops 352321536 | bytes 29491200 | tf_op jit(solution)/shard_map/while/body/eval_jaxpr/dot_general | solution.py:19
  1379.1 35.8 %all-reduce.2.cloned.1.call-done = f32[4,7168]{1,0:T(4,128)} async-done(((f32[4,7168]{1,0:T(4,128)}), f32[4,7168]{1,0:T(4,128)}) %all-reduce.2.cloned.1.call-update) | async-done | bytes 114704 | tf_op jit(solution)/shard_map/while/body/eval_jaxpr/psum | solution.py:37
  1493.8 35.8 %all-reduce.2.cloned.1.call-done = f32[4,7168]{1,0:T(4,128)} async-done(((f32[4,7168]{1,0:T(4,128)}), f32[4,7168]{1,0:T(4,128)}) %all-reduce.2.cloned.1.call-update) | async-done | bytes 114704 | tf_op jit(solution)/shard_map/while/body/eval_jaxpr/psum | solution.py:37
  1608.6 35.8 %all-reduce.2.cloned.1.call-done = f32[4,7168]{1,0:T(4,128)} async-done(((f32[4,7168]{1,0:T(4,128)}), f32[4,7168]{1,0:T(4,128)}) %all-reduce.2.cloned.1.call-update) | async-done | bytes 114704 | tf_op jit(solution)/shard_map/while/body/eval_jaxpr/psum | solution.py:37
  1723.3 35.8 %all-reduce.2.cloned.1.call-done = f32[4,7168]{1,0:T(4,128)} async-done(((f32[4,7168]{1,0:T(4,128)}), f32[4,7168]{1,0:T(4,128)}) %all-reduce.2.cloned.1.call-update) | async-done | bytes 114704 | tf_op jit(solution)/shard_map/while/body/eval_jaxpr/psum | solution.py:37
  1838.0 35.8 %all-reduce.2.cloned.1.call-done = f32[4,7168]{1,0:T(4,128)} async-done(((f32[4,7168]{1,0:T(4,128)}), f32[4,7168]{1,0:T(4,128)}) %all-reduce.2.cloned.1.call-update) | async-done | bytes 114704 | tf_op jit(solution)/shard_map/while/body/eval_jaxpr/psum | solution.py:37
  1875.1 30.4 %convolution_subtract_fusion = f32[1024,7168]{1,0:T(8,128)} fusion(f32[1024,7168]{1,0:T(8,128)} %get-tuple-element.73, f32[4,1024]{1,0:T(4,128)} %get-tuple-element.25, f32[4,7168]{1,0:T(4,128)S(1)} %get-tuple-element.22), kind=kOutput, calls=%fused_computation.12 | convolution fusion | flops 359661568 | bytes 58851328 | tf_op jit(solution)/shard_map/dot_general | solution.py:45
  (256 shorter events, 1128.2 us)
Async XLA Ops:
  7.2 31.0 %copy-start.1 = (f32[4,7168]{1,0:T(4,128)S(1)}, f32[4,7168]{1,0:T(4,128)}, u32[]{:S(2)}) copy-start(f32[4,7168]{1,0:T(4,128)} %param.7) | copy-start | bytes 344068
  38.1 114.7 %all-reduce.2.cloned.1.call-start = ((), (), s32[]{:S(2)}) async-start(), calls=%async_computation | async-start | bytes 229376 | tf_op jit(solution)/shard_map/while/body/eval_jaxpr/psum | solution.py:37
  154.1 113.5 %all-reduce.2.cloned.1.call-start = ((), (), s32[]{:S(2)}) async-start(), calls=%async_computation | async-start | bytes 229376 | tf_op jit(solution)/shard_map/while/body/eval_jaxpr/psum | solution.py:37
  268.9 113.4 %all-reduce.2.cloned.1.call-start = ((), (), s32[]{:S(2)}) async-start(), calls=%async_computation | async-start | bytes 229376 | tf_op jit(solution)/shard_map/while/body/eval_jaxpr/psum | solution.py:37
  383.6 113.4 %all-reduce.2.cloned.1.call-start = ((), (), s32[]{:S(2)}) async-start(), calls=%async_computation | async-start | bytes 229376 | tf_op jit(solution)/shard_map/while/body/eval_jaxpr/psum | solution.py:37
  498.3 113.4 %all-reduce.2.cloned.1.call-start = ((), (), s32[]{:S(2)}) async-start(), calls=%async_computation | async-start | bytes 229376 | tf_op jit(solution)/shard_map/while/body/eval_jaxpr/psum | solution.py:37
  613.1 113.4 %all-reduce.2.cloned.1.call-start = ((), (), s32[]{:S(2)}) async-start(), calls=%async_computation | async-start | bytes 229376 | tf_op jit(solution)/shard_map/while/body/eval_jaxpr/psum | solution.py:37
  727.8 113.4 %all-reduce.2.cloned.1.call-start = ((), (), s32[]{:S(2)}) async-start(), calls=%async_computation | async-start | bytes 229376 | tf_op jit(solution)/shard_map/while/body/eval_jaxpr/psum | solution.py:37
  842.5 113.4 %all-reduce.2.cloned.1.call-start = ((), (), s32[]{:S(2)}) async-start(), calls=%async_computation | async-start | bytes 229376 | tf_op jit(solution)/shard_map/while/body/eval_jaxpr/psum | solution.py:37
  957.3 113.4 %all-reduce.2.cloned.1.call-start = ((), (), s32[]{:S(2)}) async-start(), calls=%async_computation | async-start | bytes 229376 | tf_op jit(solution)/shard_map/while/body/eval_jaxpr/psum | solution.py:37
  1072.0 113.4 %all-reduce.2.cloned.1.call-start = ((), (), s32[]{:S(2)}) async-start(), calls=%async_computation | async-start | bytes 229376 | tf_op jit(solution)/shard_map/while/body/eval_jaxpr/psum | solution.py:37
  1186.7 113.4 %all-reduce.2.cloned.1.call-start = ((), (), s32[]{:S(2)}) async-start(), calls=%async_computation | async-start | bytes 229376 | tf_op jit(solution)/shard_map/while/body/eval_jaxpr/psum | solution.py:37
  1301.5 113.4 %all-reduce.2.cloned.1.call-start = ((), (), s32[]{:S(2)}) async-start(), calls=%async_computation | async-start | bytes 229376 | tf_op jit(solution)/shard_map/while/body/eval_jaxpr/psum | solution.py:37
  1416.2 113.4 %all-reduce.2.cloned.1.call-start = ((), (), s32[]{:S(2)}) async-start(), calls=%async_computation | async-start | bytes 229376 | tf_op jit(solution)/shard_map/while/body/eval_jaxpr/psum | solution.py:37
  1530.9 113.4 %all-reduce.2.cloned.1.call-start = ((), (), s32[]{:S(2)}) async-start(), calls=%async_computation | async-start | bytes 229376 | tf_op jit(solution)/shard_map/while/body/eval_jaxpr/psum | solution.py:37
  1645.7 113.4 %all-reduce.2.cloned.1.call-start = ((), (), s32[]{:S(2)}) async-start(), calls=%async_computation | async-start | bytes 229376 | tf_op jit(solution)/shard_map/while/body/eval_jaxpr/psum | solution.py:37
  1760.4 113.4 %all-reduce.2.cloned.1.call-start = ((), (), s32[]{:S(2)}) async-start(), calls=%async_computation | async-start | bytes 229376 | tf_op jit(solution)/shard_map/while/body/eval_jaxpr/psum | solution.py:37
  1875.1 30.4 %copy-start = (f32[4,7168]{1,0:T(4,128)}, f32[4,7168]{1,0:T(4,128)S(1)}, u32[]{:S(2)}) copy-start(f32[4,7168]{1,0:T(4,128)S(1)} %get-tuple-element.22) | copy-start | bytes 344068
Sparse Core Ops, SparseCore 0:
  96.4 56.3 all-reduce.1
  211.5 56.0 all-reduce.1
  326.3 55.9 all-reduce.1
  441.0 55.9 all-reduce.1
  555.7 55.9 all-reduce.1
  670.5 55.9 all-reduce.1
  785.2 55.9 all-reduce.1
  899.9 55.9 all-reduce.1
  1014.7 55.9 all-reduce.1
  1129.4 55.9 all-reduce.1
  1244.1 55.9 all-reduce.1
  1358.9 55.9 all-reduce.1
  1473.6 55.9 all-reduce.1
  1588.3 55.9 all-reduce.1
  1703.0 55.9 all-reduce.1
  1817.8 55.9 all-reduce.1
where the time goes:
time: 1910 us
  matrix products  786 us (41%)
  waiting for transfers between devices  573 us (30%)
  blocking collectives  471 us (25%)
  other arithmetic  65.4 us (3%)
    psum x16, waiting for transfers between devices, iterate(): gram, cross = lax.psum((gram_part, cross_part), 'row')  572 us
    dot_general x16, matrix products, iterate(): lax.dot_general(q_current, merged, (((1,), (1,)), ((), ())), precision=hi...  433 us
    dot_general x16, matrix products, iterate(): jnp.dot(p_factor, merged, precision=highest, preferred_element_type=jnp.f...  286 us
    psum x16, blocking collectives, iterate(): gram, cross = lax.psum((gram_part, cross_part), 'row')  274 us
    psum x16, blocking collectives, sum_over_cols(): return lax.psum(partial_value, 'col')  196 us
  transfers between devices with their start and end apart: 16, of which 16 were waited for; matrix products, arithmetic and copies ran while one was open for 3% of the time, Pallas kernels for 0%

commit v1 on v0

v1 whole, which is shorter than its diff:
```python
import functools

import jax
import jax.numpy as jnp
from jax import lax
from jax.experimental import pallas as pl
from jax.experimental.pallas import tpu as pltpu
from jax.sharding import PartitionSpec as P

ITERS = 16
MESH = pl.DeviceIdType.MESH
LANE = 128
SUB = 8


def factor(gram):
    low = [[None] * 4 for _ in range(4)]
    for i in range(4):
        for j in range(i + 1):
            rest = gram[i][j]
            for k in range(j):
                rest = rest - low[i][k] * low[j][k]
            low[i][j] = jnp.sqrt(rest) if i == j else rest / low[j][j]
    return low


def solve(low, rows):
    found = []
    for i in range(4):
        rest = rows[i]
        for k in range(i):
            rest = rest - low[i][k] * found[k]
        found.append(rest / low[i][i])
    return found


def kernel(
    n_row, n_col, chunks,
    grad_ref, res_ref, q0_ref, q_out, p_out,
    m, slot, acc, pb, qb, p_mine, p_in, p_sum, c_mine, c_in, q_all,
    g_sem, r_sem, a_send, a_recv, b_send, b_recv, c_send, c_recv,
):
    rows, cols = m.shape
    width = q_all.shape[-1]
    tiles = width // LANE
    groups = cols // width
    chunk = rows // chunks
    me_row, me_col = lax.axis_index("row"), lax.axis_index("col")
    col_peer = lambda d: (me_row, lax.rem(me_col + d, n_col))
    row_peer = lambda d: (lax.rem(me_row + d, n_row), me_col)

    barrier = pltpu.get_barrier_semaphore()
    for d in range(1, n_col):
        pl.semaphore_signal(barrier, inc=1, device_id=col_peer(d), device_id_type=MESH)
    for d in range(1, n_row):
        pl.semaphore_signal(barrier, inc=1, device_id=row_peer(d), device_id_type=MESH)

    def grad_copy(i):
        part = pl.ds(i * chunk, chunk)
        return pltpu.make_async_copy(grad_ref.at[part], m.at[part], g_sem.at[i])

    def res_copy(i):
        part = pl.ds(i * chunk, chunk)
        return pltpu.make_async_copy(res_ref.at[part], slot.at[i % 2], r_sem.at[i % 2])

    for i in range(chunks):
        grad_copy(i).start()
        if i < 2:
            res_copy(i).start()
    for g in range(groups):
        part = slice(g * width, (g + 1) * width)
        q_now = q0_ref[:, part]
        for r in range(4):
            qb[r, :, part] = jnp.broadcast_to(q_now[r : r + 1], (SUB, width))
    c_mine[...] = jnp.zeros_like(c_mine)
    for i in range(chunks):
        grad_copy(i).wait()
        res_copy(i).wait()

        @pl.loop(0, chunk // SUB)
        def _(k):
            here = pl.ds(pl.multiple_of(i * chunk + k * SUB, SUB), SUB)
            m[here, :] += slot[i % 2, pl.ds(pl.multiple_of(k * SUB, SUB), SUB), :]

        if i + 2 < chunks:
            res_copy(i + 2).start()
    pl.semaphore_wait(barrier, n_col + n_row - 2)

    high = 32

    def iterate(step, carry):
        par = lax.rem(step, 2)

        @pl.loop(0, rows // high)
        def _(k):
            here = pl.ds(pl.multiple_of(k * high, high), high)
            totals = [jnp.zeros((high // SUB, SUB, LANE), jnp.float32)] * 4
            for c in range(cols // LANE):
                part = slice(c * LANE, (c + 1) * LANE)
                piece = m[here, part].reshape(high // SUB, SUB, LANE)
                for r in range(4):
                    totals[r] = totals[r] + piece * qb[r, :, part][None]
            for r in range(4):
                acc[r, here, :] = totals[r].reshape(high, LANE)

        for b in range(rows // LANE):
            part = slice(b * LANE, (b + 1) * LANE)
            sums = [jnp.sum(acc[r, part, :].T, axis=0, keepdims=True) for r in range(4)]
            p_mine[0, :, part] = jnp.concatenate(sums, axis=0)

        def p_copy(d):
            return pltpu.make_async_remote_copy(
                src_ref=p_mine.at[0], dst_ref=p_in.at[par, d],
                send_sem=a_send.at[d], recv_sem=a_recv.at[par, d],
                device_id=col_peer(d), device_id_type=MESH,
            )

        for d in range(1, n_col):
            p_copy(d).start()
        for d in range(1, n_col):
            p_copy(d).wait()
        p_now = p_mine[0]
        for d in range(1, n_col):
            p_now = p_now + p_in[par, d]
        p_sum[0] = p_now

        row_id = lax.broadcasted_iota(jnp.int32, (4, LANE), 0)
        lane_id = lax.broadcasted_iota(jnp.int32, (4, LANE), 1)
        corner = jnp.zeros((4, LANE), jnp.float32)
        for i in range(4):
            dots = jnp.sum(p_now * p_now[i : i + 1], axis=1, keepdims=True)
            corner = jnp.where(lane_id == i, dots, corner)
        for s in range(n_row):
            c_mine[s, :, width:] = corner
        for r in range(4):
            for b in range(rows // LANE):
                part = slice(b * LANE, (b + 1) * LANE)
                pb[r, part, :] = jnp.broadcast_to(p_now[r : r + 1, part], (LANE, LANE)).T

        @pl.loop(0, groups)
        def _(g):
            def add(k, totals):
                totals = list(totals)
                for u in range(high // SUB):
                    here = pl.ds(pl.multiple_of(k * high + u * SUB, SUB), SUB)
                    scale = [pb[r, here, :] for r in range(4)]
                    for t in range(tiles):
                        piece = m[here, pl.ds(pl.multiple_of(g * width + t * LANE, LANE), LANE)]
                        for r in range(4):
                            totals[r * tiles + t] = totals[r * tiles + t] + piece * scale[r]
                return tuple(totals)

            start = (jnp.zeros((SUB, LANE), jnp.float32),) * (4 * tiles)
            totals = lax.fori_loop(0, rows // high, add, start)
            for t in range(tiles):
                sums = [
                    jnp.sum(totals[r * tiles + t], axis=0, keepdims=True) for r in range(4)
                ]
                c_mine[g, :, t * LANE : (t + 1) * LANE] = jnp.concatenate(sums, axis=0)

        def c_copy(d):
            return pltpu.make_async_remote_copy(
                src_ref=c_mine.at[lax.rem(me_row + d, n_row)], dst_ref=c_in.at[par, d],
                send_sem=b_send.at[d], recv_sem=b_recv.at[par, d],
                device_id=row_peer(d), device_id_type=MESH,
            )

        for d in range(1, n_row):
            c_copy(d).start()
        for d in range(1, n_row):
            c_copy(d).wait()
        cross = c_mine[me_row]
        for d in range(1, n_row):
            cross = cross + c_in[par, d]
        gram = [
            [cross[i : i + 1, width + j : width + j + 1] for j in range(4)] for i in range(4)
        ]
        low = factor(gram)
        q_rows = solve(low, [cross[r : r + 1, :width] for r in range(4)])
        q_all[par, me_row] = jnp.concatenate(q_rows, axis=0)

        def q_copy(d):
            mine = q_all.at[par, me_row]
            return pltpu.make_async_remote_copy(
                src_ref=mine, dst_ref=mine,
                send_sem=c_send.at[d], recv_sem=c_recv.at[par, d],
                device_id=row_peer(d), device_id_type=MESH,
            )

        for d in range(1, n_row):
            q_copy(d).start()
        p_held = p_sum[0]
        p_rows = solve(low, [p_held[r : r + 1] for r in range(4)])
        p_out[...] = jnp.concatenate(p_rows + p_rows, axis=0)
        for d in range(1, n_row):
            q_copy(d).wait()
        for g in range(groups):
            q_now = q_all[par, g]
            for r in range(4):
                qb[r, :, g * width : (g + 1) * width] = jnp.broadcast_to(
                    q_now[r : r + 1], (SUB, width)
                )
        return carry

    lax.fori_loop(0, ITERS, iterate, 0)
    for g in range(groups):
        q_now = q_all[(ITERS - 1) % 2, g]
        q_out[:, g * width : (g + 1) * width] = jnp.concatenate([q_now, q_now], axis=0)


def shards(n_row, n_col, gradient, residual, q_init):
    rows, cols = gradient.shape
    width = -(-cols // (LANE * n_row)) * LANE
    chunks = 8
    f32 = jnp.float32
    vmem = lambda *shape: pltpu.VMEM(shape, f32)
    dma = pltpu.SemaphoreType.DMA
    q_wide, p_basis = pl.pallas_call(
        functools.partial(kernel, n_row, n_col, chunks),
        out_shape=(
            jax.ShapeDtypeStruct((SUB, cols), f32),
            jax.ShapeDtypeStruct((SUB, rows), f32),
        ),
        in_specs=[
            pl.BlockSpec(memory_space=pl.ANY),
            pl.BlockSpec(memory_space=pl.ANY),
            pl.BlockSpec(memory_space=pltpu.VMEM),
        ],
        out_specs=(
            pl.BlockSpec(memory_space=pltpu.VMEM),
            pl.BlockSpec(memory_space=pltpu.VMEM),
        ),
        scratch_shapes=[
            vmem(rows, cols),
            vmem(2, rows // chunks, cols),
            vmem(4, rows, LANE),
            vmem(4, rows, LANE),
            vmem(4, SUB, cols),
            vmem(3, 4, rows),
            vmem(3, n_col, 4, rows),
            vmem(3, 4, rows),
            vmem(n_row + 2, 4, width + LANE),
            vmem(3, n_row, 4, width + LANE),
            vmem(3, n_row, 4, width),
            dma((chunks,)),
            dma((2,)),
            dma((n_col,)),
            dma((2, n_col)),
            dma((n_row,)),
            dma((2, n_row)),
            dma((n_row,)),
            dma((2, n_row)),
        ],
        compiler_params=pltpu.CompilerParams(
            collective_id=0, has_side_effects=True, vmem_limit_bytes=60 * 1024 * 1024
        ),
    )(gradient, residual, jnp.pad(q_init, ((0, SUB - 4), (0, 0))))
    q_factor = q_wide[:4]
    left = gradient + residual
    for r in range(4):
        left = left - p_basis[r][:, None] * q_factor[r][None, :]
    return (q_factor, left)


def solution(mesh):
    in_specs = (P("row", "col"), P("row", "col"), P(None, "col"))
    out_specs = (P(None, "col"), P("row", "col"))
    body = functools.partial(shards, mesh.shape["row"], mesh.shape["col"])
    return jax.shard_map(body, mesh=mesh, in_specs=in_specs, out_specs=out_specs, check_vma=False)
```

time: 1910 us -> 601 us (0.31)
  matrix products: 786 us -> 0 us
  waiting for transfers between devices: 573 us -> 0 us
  Pallas kernels: 0 us -> 564 us
  blocking collectives: 471 us -> 0 us
  other arithmetic: 65.4 us -> 29.7 us
    dot_general x49 -> x0, matrix products: 752 us -> none  [the longest x16 433 us: iterate(): lax.dot_general(q_current, merged, (((1,), (1,)), ((), ())), precision=hi...]
    psum x16 -> x0, waiting for transfers between devices: 572 us -> none  [iterate(): gram, cross = lax.psum((gram_part, cross_part), 'row')]
    pallas_call x0 -> x1, Pallas kernels: none -> 564 us  [shards(): pl.pallas_call(functools.partial(kernel, n_row, n_col, chunks), out_shape...]
    psum x32 -> x0, blocking collectives: 471 us -> none  [the longest x16 274 us: iterate(): gram, cross = lax.psum((gram_part, cross_part), 'row')]
    another operation x80 -> x0, other arithmetic: 34.4 us -> none  [the longest x48 17.8 us: iterate(): factor_low = jnp.linalg.cholesky(gram)]
    another operation x32 -> x0, matrix products: 34.2 us -> none  [the longest x16 20.7 us: iterate(): q_next = jax.scipy.linalg.solve_triangular(factor_low, cross, lower=True)]
    add x1 -> x0, other arithmetic: 30.9 us -> none  [shards(): merged = gradient + residual]
    sub x0 -> x1, other arithmetic: none -> 29.7 us  [shards(): left = left - p_basis[r][:, None] * q_factor[r][None, :]]
  transfers between devices with their start and end apart: 16 -> 0, of which waited for: 16 -> 0; matrix products, arithmetic and copies ran while one was open for 3% -> 0% of each run, Pallas kernels for 0% -> 0%
where the time goes in v1:
time: 601 us; the launch traced here: 600 us
  Pallas kernels  564 us (94%)
  other arithmetic  29.7 us (5%)
    pallas_call x1, Pallas kernels, shards(): pl.pallas_call(functools.partial(kernel, n_row, n_col, chunks), out_shape...  564 us
    sub x1, other arithmetic, shards(): left = left - p_basis[r][:, None] * q_factor[r][None, :]  29.7 us

profile of v1, /device:TPU:1, one launch (start us, length us, event | category | flops | bytes accessed | tf_op | source)
XLA Modules:
  0.0 599.9 jit_solution(5993107907958767958)
XLA Ops:
  0.6 1.6 pad.4.q0_ref
  2.2 564.1 %shard_map.50 = (f32[8,7168]{1,0:T(8,128)}, f32[8,1024]{1,0:T(8,128)}) custom-call(f32[1024,7168]{1,0:T(8,128)} %grad_ref.1, f32[1024,7168]{1,0:T(8,128)} %res_ref.1, f32[8,7168]{1,0:T(8,128)} %pad.4.q0_ref), custom_call_target="tpu_custom_call" | custom-call | tf_op jit(solution)/shard_map/pallas_call | solution.py:218
  566.4 0.9 fusion.1
  567.3 1.6 slice.31
  568.9 1.4 fusion
  570.3 29.7 %multiply_subtract_fusion = f32[1024,7168]{1,0:T(8,128)} fusion(f32[1024,7168]{1,0:T(8,128)} %grad_ref.1, f32[1024,7168]{1,0:T(8,128)} %res_ref.1, f32[7168]{0:T(1024)S(1)} %bitcast.9, f32[1024]{0:T(1024)S(1)} %bitcast.13, f32[7168]{0:T(1024)S(1)} %bitcast.10, f32[1024]{0:T(1024)S(1)} %bitcast.14, f32[7168]{0:T(1024)S(1)} %bitcast.11, f32[1024]{0:T(1024)S(1)} %bitcast.15, ...), kind=kLoop, calls=%fused_computation | loop fusion | flops 66060288 | bytes 88211456 | tf_op jit(solution)/shard_map/sub | solution.py:261
